TPU v7x, 32 devices: a whole 2x2x4 slice. The times are simulated.
32 devices in a mesh: groups: 2 (over y), slab: 4 (over z), pencil: 2 (over x), comp: 2 (over core).
Axes of the slice: x: 2, y: 2, z: 4, core: 2. Of those that a mesh axis runs over, the one named last changes fastest.
Arguments:
- u_start: float32 [3, 64, 64, 512], P(None, ('groups', 'slab'), 'pencil', 'comp'), parts along dimension 1, may hold values from -6 to 6
- toughness: float32 [64, 64, 512], P(('groups', 'slab'), 'pencil', 'comp'), parts along dimension 0, may hold values from 0.3 to 1.5
- crack_label: int32 [64, 64, 512], P(('groups', 'slab'), 'pencil', 'comp'), parts along dimension 0, may hold values from 0 to 2
- obs_weight: bfloat16 [32, 64, 2, 4096], P('slab', 'pencil', 'comp'), may hold values from -0.75 to 0.75
- sensor_cell: int32 [4096], replicated, may hold values from 0 to 4095
Outputs:
- moved: float32 [3, 64, 64, 512], P(None, ('groups', 'slab'), 'pencil', 'comp'), parts along dimension 1
- damage: float32 [64, 64, 512], P(('groups', 'slab'), 'pencil', 'comp'), parts along dimension 0
- readings: float32 [3, 8192], P(None, 'groups'), parts along dimension 1
There are 2 independent parts, one for each index of `groups`. A program takes and returns all parts, laid end to end along the dimension named above; an argument that names none is the same for every part. Nothing has to cross between parts.
Inputs may be any that keep to these rules, and one draw needn't show every extreme that they name: `sensor_cell`: numbers cell blocks as (64 z + y) * 2 + h. `crack_label`: 0 intact, 1 partly cracked, 2 cracked.
All inputs are finite; a program needn't handle non-finite values.
Results may differ from a plain program's by a relative error of at most 0.003.
Values sent between devices are 32-bit elements; how exact they have to be, the bound alone decides.
A program may use at most 128 MiB of HBM per device.

v0:
```python
import jax
import jax.numpy as jnp
from jax import lax
from jax.sharding import PartitionSpec as P

SHEAR_MODULUS = 1.0
LAME_FIRST = 1.5
RESIDUAL_STIFF = 0.001
TIME_DISP = 0.15
TIME_DAMAGE = 0.08
LENGTH_SCALE = 1.0
DAMAGE_LEVEL = 0.45
POINT_GAIN = 8.0


def with_halo(block, sides, width):
    for axis, dim in sides:
        count = lax.axis_size(axis)
        forward = [(i, i + 1) for i in range(count - 1)]
        backward = [(target, source) for source, target in forward]
        low = lax.ppermute(
            lax.slice_in_dim(block, block.shape[dim] - width, None, axis=dim), axis, forward
        )
        high = lax.ppermute(lax.slice_in_dim(block, 0, width, axis=dim), axis, backward)
        block = jnp.concatenate([low, block, high], axis=dim)
    return block


def central(source, spatial):
    if spatial == 0:
        return 0.5 * (source[..., 2:, 1:-1, 1:-1] - source[..., :-2, 1:-1, 1:-1])
    if spatial == 1:
        return 0.5 * (source[..., 1:-1, 2:, 1:-1] - source[..., 1:-1, :-2, 1:-1])
    return 0.5 * (source[..., 1:-1, 1:-1, 2:] - source[..., 1:-1, 1:-1, :-2])


def shrink(source):
    return source[..., 1:-1, 1:-1, 1:-1]


def laplace(source):
    return (
        source[2:, 1:-1, 1:-1]
        + source[:-2, 1:-1, 1:-1]
        + source[1:-1, 2:, 1:-1]
        + source[1:-1, :-2, 1:-1]
        + source[1:-1, 1:-1, 2:]
        + source[1:-1, 1:-1, :-2]
        - 6.0 * source[1:-1, 1:-1, 1:-1]
    )


def entry_key(first, second):
    return (min(first, second), max(first, second))


def rotate(matrix, first, second):
    other = 3 - first - second
    diag_first = matrix[first, first]
    diag_second = matrix[second, second]
    coupling = matrix[first, second]
    angle = 0.5 * jnp.arctan2(2.0 * coupling, diag_second - diag_first)
    cosine = jnp.cos(angle)
    sine = jnp.sin(angle)
    side_first = matrix[entry_key(other, first)]
    side_second = matrix[entry_key(other, second)]
    result = dict(matrix)
    result[first, first] = (
        cosine * cosine * diag_first - 2.0 * cosine * sine * coupling + sine * sine * diag_second
    )
    result[second, second] = (
        sine * sine * diag_first + 2.0 * cosine * sine * coupling + cosine * cosine * diag_second
    )
    result[first, second] = jnp.zeros_like(coupling)
    result[entry_key(other, first)] = cosine * side_first - sine * side_second
    result[entry_key(other, second)] = sine * side_first + cosine * side_second
    return result


def eigenvalues(matrix):
    for sweep_index in range(5):
        for first, second in ((0, 1), (0, 2), (1, 2)):
            matrix = rotate(matrix, first, second)
    return [matrix[0, 0], matrix[1, 1], matrix[2, 2]]


def advance(padded_disp, padded_damage, toughness):
    gradient = [
        [central(padded_disp[component], direction) for direction in range(3)]
        for component in range(3)
    ]
    strain = {}
    for first in range(3):
        for second in range(first, 3):
            strain[first, second] = 0.5 * (gradient[first][second] + gradient[second][first])
    trace_full = strain[0, 0] + strain[1, 1] + strain[2, 2]
    damage_mid = shrink(padded_damage)
    degrade = (1.0 - damage_mid) ** 2 + RESIDUAL_STIFF
    divergence = []
    for component in range(3):
        total_force = 0.0
        for direction in range(3):
            stress = 2.0 * SHEAR_MODULUS * strain[entry_key(component, direction)]
            if component == direction:
                stress = stress + LAME_FIRST * trace_full
            total_force = total_force + central(degrade * stress, direction)
        divergence.append(total_force)
    moved = shrink(shrink(padded_disp)) + TIME_DISP * jnp.stack(divergence)
    inner = {key_pair: shrink(entry_value) for key_pair, entry_value in strain.items()}
    trace_inner = shrink(trace_full)
    energy = 0.5 * LAME_FIRST * jnp.maximum(trace_inner, 0.0) ** 2
    for eigen_value in eigenvalues(inner):
        energy = energy + SHEAR_MODULUS * jnp.maximum(eigen_value, 0.0) ** 2
    damage_core = shrink(damage_mid)
    damage = damage_core + TIME_DAMAGE * (
        2.0 * (1.0 - damage_core) * energy
        - toughness / LENGTH_SCALE * damage_core
        + toughness * LENGTH_SCALE * laplace(damage_mid)
    )
    return (moved, damage)


def local(u_start, toughness, crack_label, obs_weight, sensor_cell):
    planes, rows, columns = toughness.shape
    damage = DAMAGE_LEVEL * crack_label.astype(jnp.float32)
    moved = u_start
    for repeat in range(2):
        stacked = jnp.concatenate([moved, damage[None]], axis=0)
        padded = with_halo(stacked, (("slab", 1), ("pencil", 2), ("comp", 3)), 2)
        moved, damage = advance(padded[:3], padded[3], toughness)
    pooled = jnp.mean(moved, axis=-1).reshape(3, planes * rows).astype(jnp.bfloat16)
    weight_rows = obs_weight.reshape(planes * rows, obs_weight.shape[-1])
    dense = jnp.dot(pooled, weight_rows, preferred_element_type=jnp.float32)
    plane_ids = lax.axis_index("slab") * planes + jnp.arange(planes, dtype=jnp.int32)
    row_ids = lax.axis_index("pencil") * rows + jnp.arange(rows, dtype=jnp.int32)
    block_ids = (
        (plane_ids[:, None] * (rows * lax.axis_size("pencil")) + row_ids[None, :])
        * lax.axis_size("comp")
        + lax.axis_index("comp")
    ).reshape(planes * rows)
    picks = (block_ids[:, None] == sensor_cell[None, :]).astype(jnp.bfloat16)
    point = jnp.dot(pooled, picks, preferred_element_type=jnp.float32)
    partial_sum = dense + POINT_GAIN * point
    readings = lax.psum(partial_sum, ("slab", "pencil", "comp"))
    return (moved, damage, readings)


def solution(mesh):
    return jax.shard_map(
        local,
        mesh=mesh,
        in_specs=(
            P(None, ("groups", "slab"), "pencil", "comp"),
            P(("groups", "slab"), "pencil", "comp"),
            P(("groups", "slab"), "pencil", "comp"),
            P("slab", "pencil", "comp", None),
            P(),
        ),
        out_specs=(
            P(None, ("groups", "slab"), "pencil", "comp"),
            P(("groups", "slab"), "pencil", "comp"),
            P(None, "groups"),
        ),
        check_vma=False,
    )
```

profile of v0, /device:TPU:0, one launch (start us, length us, event | category | flops | bytes accessed | tf_op | source)
XLA Modules:
  0.0 226.6 jit_solution(18250146474018214217)
XLA Ops:
  2.9 5.0 %collective-permute-start = (f32[4,2,32,256]{3,2,1,0:T(8,128)S(1)}, f32[4,2,32,256]{3,2,1,0:T(8,128)S(1)}, u32[]{:S(2)}, u32[]{:S(2)}) collective-permute-start(f32[4,2,32,256]{3,2,1,0:T(8,128)S(1)} %get-tuple-element.66), channel_id=1, source_target_pairs={{0,4},{4,8},{8,12},{1,5},{5,9},{9,13},{2,6},{6,10},{10,14},{3,7},{... | collective-permute-start | bytes 786440 | tf_op jit(solution)/shard_map/ppermute | solution.py:21
  9.1 4.2 %collective-permute-done = f32[4,2,32,256]{3,2,1,0:T(8,128)S(1)} collective-permute-done((f32[4,2,32,256]{3,2,1,0:T(8,128)S(1)}, f32[4,2,32,256]{3,2,1,0:T(8,128)S(1)}, u32[]{:S(2)}, u32[]{:S(2)}) %collective-permute-start) | collective-permute-done | bytes 262176 | tf_op jit(solution)/shard_map/ppermute | solution.py:21
  13.4 4.1 %collective-permute-done.1 = f32[4,2,32,256]{3,2,1,0:T(8,128)S(1)} collective-permute-done((f32[4,2,32,256]{3,2,1,0:T(8,128)S(1)}, f32[4,2,32,256]{3,2,1,0:T(8,128)S(1)}, u32[]{:S(2)}, u32[]{:S(2)}) %collective-permute-start.1) | collective-permute-done | bytes 262176 | tf_op jit(solution)/shard_map/ppermute | solution.py:24
  18.7 3.4 %collective-permute-start.2 = (f32[4,12,2,256]{3,2,1,0:T(2,128)S(1)}, f32[4,12,2,256]{3,2,1,0:T(2,128)S(1)}, u32[]{:S(2)}, u32[]{:S(2)}) collective-permute-start(f32[4,12,2,256]{3,2,1,0:T(2,128)S(1)} %get-tuple-element.58), channel_id=1, source_target_pairs={{0,2},{1,3},{4,6},{5,7},{8,10},{9,11},{12,14},{13,15},{16,18},{17,... | collective-permute-start | bytes 294920 | tf_op jit(solution)/shard_map/ppermute | solution.py:21
  24.3 4.3 %collective-permute-done.3 = f32[4,12,2,256]{3,2,1,0:T(2,128)S(1)} collective-permute-done((f32[4,12,2,256]{3,2,1,0:T(2,128)S(1)}, f32[4,12,2,256]{3,2,1,0:T(2,128)S(1)}, u32[]{:S(2)}, u32[]{:S(2)}) %collective-permute-start.3) | collective-permute-done | bytes 98336 | tf_op jit(solution)/shard_map/ppermute | solution.py:24
  28.9 1.6 fusion.80
  30.5 1.6 copy.24
  32.2 1.9 collective-permute-start.4
  34.1 2.2 copy.25
  37.6 2.2 copy.26
  39.8 2.2 copy.27
  42.0 3.1 %pad_maximum_fusion = f32[4,12,36,260]{3,2,1,0:T(8,128)S(1)} fusion(f32[4,12,36,2]{3,2,1,0:T(8,128)} %copy.27, f32[4,12,2,256]{3,2,1,0:T(2,128)} %copy-done.13, f32[4,2,32,256]{3,2,1,0:T(8,128)} %copy-done.5, f32[1,8,32,256]{3,2,1,0:T(8,128)S(1)} %multiply_bitcast_fusion, f32[3,8,32,256]{3,2,1,0:T(8,128)S(1)} %copy-done.1, ...), kind=kLoop, calls=%fused_computation.3 | loop fusion | flops 3144960 | bytes 3594240 | tf_op jit(solution)/shard_map/concatenate | solution.py:25
  45.3 2.2 multiply_multiply_fusion.5
  50.1 29.3 %fusion.51 = f32[1,8,32,256]{3,2,1,0:T(8,128)S(1)} fusion(f32[8,32,256]{2,1,0:T(8,128)S(1)} %copy-done.15, f32[12,36,260]{2,1,0:T(8,128)S(1)} %get-tuple-element.37, f32[10,34,258]{2,1,0:T(8,128)S(1)} %get-tuple-element.46, f32[10,34,258]{2,1,0:T(8,128)S(1)} %get-tuple-element.47, f32[10,34,258]{2,1,0:T(8,128)S(1)} %get-tuple-element.29, ...), kind=kLoop, calls=%fused_computation.127 | loop fusion | flops 23068672 | bytes 4194304 | tf_op jit(solution)/shard_map/broadcast_in_dim | solution.py:128
  80.3 3.5 %collective-permute-start.6 = (f32[4,2,32,256]{3,2,1,0:T(8,128)}, f32[4,2,32,256]{3,2,1,0:T(8,128)S(1)}, u32[]{:S(2)}, u32[]{:S(2)}) collective-permute-start(f32[4,2,32,256]{3,2,1,0:T(8,128)} %get-tuple-element.64), channel_id=1, source_target_pairs={{0,4},{4,8},{8,12},{1,5},{5,9},{9,13},{2,6},{6,10},{10,14},{3,7},{... | collective-permute-start | bytes 786440 | tf_op jit(solution)/shard_map/ppermute | solution.py:21
  85.7 4.3 %collective-permute-done.6 = f32[4,2,32,256]{3,2,1,0:T(8,128)S(1)} collective-permute-done((f32[4,2,32,256]{3,2,1,0:T(8,128)}, f32[4,2,32,256]{3,2,1,0:T(8,128)S(1)}, u32[]{:S(2)}, u32[]{:S(2)}) %collective-permute-start.6) | collective-permute-done | bytes 262176 | tf_op jit(solution)/shard_map/ppermute | solution.py:21
  90.0 4.7 %collective-permute-done.7 = f32[4,2,32,256]{3,2,1,0:T(8,128)} collective-permute-done((f32[4,2,32,256]{3,2,1,0:T(8,128)}, f32[4,2,32,256]{3,2,1,0:T(8,128)}, u32[]{:S(2)}, u32[]{:S(2)}) %collective-permute-start.7) | collective-permute-done | bytes 262176 | tf_op jit(solution)/shard_map/ppermute | solution.py:24
  95.9 1.5 collective-permute-start.8
  100.0 4.1 %collective-permute-done.9 = f32[4,12,2,256]{3,2,1,0:T(2,128)S(1)} collective-permute-done((f32[4,12,2,256]{3,2,1,0:T(2,128)S(1)}, f32[4,12,2,256]{3,2,1,0:T(2,128)S(1)}, u32[]{:S(2)}, u32[]{:S(2)}) %collective-permute-start.9) | collective-permute-done | bytes 98336 | tf_op jit(solution)/shard_map/ppermute | solution.py:24
  104.1 1.5 pad_maximum_fusion.3
  105.6 1.6 fusion.79
  107.2 1.6 copy.28
  108.8 1.9 collective-permute-start.10
  110.7 2.2 copy.29
  117.0 2.2 copy.30
  119.2 2.2 copy.31
  121.4 3.3 %pad_maximum_fusion.1 = f32[4,12,36,260]{3,2,1,0:T(8,128)S(1)} fusion(f32[4,12,36,2]{3,2,1,0:T(8,128)} %copy.31, f32[4,12,2,256]{3,2,1,0:T(2,128)} %copy-done.12, f32[4,2,32,256]{3,2,1,0:T(8,128)} %collective-permute-done.7, f32[1,8,32,256]{3,2,1,0:T(8,128)S(1)} %fusion.51, f32[3,8,32,256]{3,2,1,0:T(8,128)} %copy-done.2, ...), kind=kLoop, calls=%fused_computation.4 | loop fusion | flops 3144960 | bytes 3594240 | tf_op jit(solution)/shard_map/concatenate | solution.py:25
  124.9 3.8 %multiply_multiply_fusion.2 = (f32[10,34,258]{2,1,0:T(8,128)S(1)}, f32[10,34,258]{2,1,0:T(8,128)}, f32[10,34,258]{2,1,0:T(8,128)S(1)}, f32[10,34,258]{2,1,0:T(8,...) fusion(f32[12,36,260]{2,1,0:T(8,128)S(1)} %get-tuple-element.33, ...), kind=kLoop, calls=%fused_computation.61 | loop fusion | flops 2456160 | bytes 8421120 | tf_op jit(solution)/shard_map/mul | solution.py:106
  128.7 2.1 multiply_multiply_fusion
  133.6 1.4 fusion
  135.0 60.5 %psum.7 = f32[3,4096]{1,0:T(4,128)} all-reduce(f32[3,4096]{1,0:T(4,128)} %fusion), channel_id=1, replica_groups=mesh['groups'=2,'slab'=4,'pencil'=2,'comp'=2] {'slab','pencil','comp'}, use_global_device_ids=true, to_apply=%region_1.0 | all-reduce | flops 12288 | bytes 98304 | tf_op jit(solution)/shard_map/psum | solution.py:144
  195.5 31.0 %fusion.26 = f32[8,32,256]{2,1,0:T(8,128)} fusion(f32[8,32,256]{2,1,0:T(8,128)} %param.6, f32[12,36,260]{2,1,0:T(8,128)S(1)} %copy-done.4, f32[10,34,258]{2,1,0:T(8,128)S(1)} %get-tuple-element.39, f32[10,34,258]{2,1,0:T(8,128)} %get-tuple-element.40, f32[10,34,258]{2,1,0:T(8,128)} %get-tuple-element.18, f32[10,34,258]{2,1,0:T(8,128)} %get-tuple-element.44, ...), kind=kLoop, calls=%fused_computation.82 | loop fusion | flops 23068672 | bytes 4194304 | tf_op jit(solution)/shard_map/add | solution.py:115
  (66 shorter events, 24.4 us)
Async XLA Ops:
  0.6 132.5 %copy-start = (bf16[8,32,1,4096]{3,1,2,0:T(8,128)(2,1)S(1)}, bf16[8,32,1,4096]{3,1,2,0:T(8,128)(2,1)}, u32[]{:S(2)}) copy-start(bf16[8,32,1,4096]{3,1,2,0:T(8,128)(2,1)} %param.8) | copy-start | bytes 6291460
  0.6 28.0 %copy-start.1 = (f32[3,8,32,256]{3,2,1,0:T(8,128)S(1)}, f32[3,8,32,256]{3,2,1,0:T(8,128)}, u32[]{:S(2)}) copy-start(f32[3,8,32,256]{3,2,1,0:T(8,128)} %param.5) | copy-start | bytes 2359300
  2.9 10.5 %collective-permute-start = (f32[4,2,32,256]{3,2,1,0:T(8,128)S(1)}, f32[4,2,32,256]{3,2,1,0:T(8,128)S(1)}, u32[]{:S(2)}, u32[]{:S(2)}) collective-permute-start(f32[4,2,32,256]{3,2,1,0:T(8,128)S(1)} %get-tuple-element.66), channel_id=1, source_target_pairs={{0,4},{4,8},{8,12},{1,5},{5,9},{9,13},{2,6},{6,10},{10,14},{3,7},{... | collective-permute-start | bytes 786440 | tf_op jit(solution)/shard_map/ppermute | solution.py:21
  7.8 9.7 %collective-permute-start.1 = (f32[4,2,32,256]{3,2,1,0:T(8,128)S(1)}, f32[4,2,32,256]{3,2,1,0:T(8,128)S(1)}, u32[]{:S(2)}, u32[]{:S(2)}) collective-permute-start(f32[4,2,32,256]{3,2,1,0:T(8,128)S(1)} %get-tuple-element.67), channel_id=1, source_target_pairs={{4,0},{8,4},{12,8},{5,1},{9,5},{13,9},{6,2},{10,6},{14,10},{7,3},{... | collective-permute-start | bytes 786440 | tf_op jit(solution)/shard_map/ppermute | solution.py:24
  17.5 13.0 %copy-start.5 = (f32[4,2,32,256]{3,2,1,0:T(8,128)}, f32[4,2,32,256]{3,2,1,0:T(8,128)S(1)}, u32[]{:S(2)}) copy-start(f32[4,2,32,256]{3,2,1,0:T(8,128)S(1)} %collective-permute-done.1) | copy-start | bytes 786436
  18.7 5.6 %collective-permute-start.2 = (f32[4,12,2,256]{3,2,1,0:T(2,128)S(1)}, f32[4,12,2,256]{3,2,1,0:T(2,128)S(1)}, u32[]{:S(2)}, u32[]{:S(2)}) collective-permute-start(f32[4,12,2,256]{3,2,1,0:T(2,128)S(1)} %get-tuple-element.58), channel_id=1, source_target_pairs={{0,2},{1,3},{4,6},{5,7},{8,10},{9,11},{12,14},{13,15},{16,18},{17,... | collective-permute-start | bytes 294920 | tf_op jit(solution)/shard_map/ppermute | solution.py:21
  22.1 6.5 %collective-permute-start.3 = (f32[4,12,2,256]{3,2,1,0:T(2,128)S(1)}, f32[4,12,2,256]{3,2,1,0:T(2,128)S(1)}, u32[]{:S(2)}, u32[]{:S(2)}) collective-permute-start(f32[4,12,2,256]{3,2,1,0:T(2,128)S(1)} %get-tuple-element.59), channel_id=1, source_target_pairs={{2,0},{3,1},{6,4},{7,5},{10,8},{11,9},{14,12},{15,13},{18,16},{19,... | collective-permute-start | bytes 294920 | tf_op jit(solution)/shard_map/ppermute | solution.py:24
  28.6 1.9 copy-start.13
  32.2 5.4 %collective-permute-start.4 = (f32[4,12,36,2]{2,0,3,1:T(4,128)S(1)}, f32[4,12,36,2]{2,0,3,1:T(4,128)}, u32[]{:S(2)}, u32[]{:S(2)}) collective-permute-start(f32[4,12,36,2]{2,0,3,1:T(4,128)S(1)} %copy.24), channel_id=1, source_target_pairs={{0,1},{2,3},{4,5},{6,7},{8,9},{10,11},{12,13},{14,15},{16,17},{18,... | collective-permute-start | bytes 41480 | tf_op jit(solution)/shard_map/ppermute | solution.py:21
  36.3 3.5 %collective-permute-start.5 = (f32[4,12,36,2]{2,0,3,1:T(4,128)}, f32[4,12,36,2]{2,0,3,1:T(4,128)}, u32[]{:S(2)}, u32[]{:S(2)}) collective-permute-start(f32[4,12,36,2]{2,0,3,1:T(4,128)} %copy.25), channel_id=1, source_target_pairs={{1,0},{3,2},{5,4},{7,6},{9,8},{11,10},{13,12},{15,14},{17,16},{19,... | collective-permute-start | bytes 41480 | tf_op jit(solution)/shard_map/ppermute | solution.py:24
  48.8 1.3 copy-start.15
  49.9 29.5 %copy-start.6 = (f32[1,8,32,256]{3,2,1,0:T(8,128)}, f32[1,8,32,256]{3,2,1,0:T(8,128)S(1)}, u32[]{:S(2)}) copy-start(f32[1,8,32,256]{3,2,1,0:T(8,128)S(1)} %get-tuple-element.71) | copy-start | bytes 786436
  49.9 29.5 %copy-start.8 = (f32[1,8,32,256]{3,2,1,0:T(8,128)}, f32[1,8,32,256]{3,2,1,0:T(8,128)S(1)}, u32[]{:S(2)}) copy-start(f32[1,8,32,256]{3,2,1,0:T(8,128)S(1)} %get-tuple-element.72) | copy-start | bytes 786436
  50.0 29.5 %copy-start.10 = (f32[1,8,32,256]{3,2,1,0:T(8,128)}, f32[1,8,32,256]{3,2,1,0:T(8,128)S(1)}, u32[]{:S(2)}) copy-start(f32[1,8,32,256]{3,2,1,0:T(8,128)S(1)} %get-tuple-element.73) | copy-start | bytes 786436
  50.1 30.2 %copy-start.2 = (f32[3,8,32,256]{3,2,1,0:T(8,128)}, f32[3,8,32,256]{3,2,1,0:T(8,128)S(1)}, u32[]{:S(2)}) copy-start(f32[3,8,32,256]{3,2,1,0:T(8,128)S(1)} %fusion.4) | copy-start | bytes 2359300
  80.3 9.7 %collective-permute-start.6 = (f32[4,2,32,256]{3,2,1,0:T(8,128)}, f32[4,2,32,256]{3,2,1,0:T(8,128)S(1)}, u32[]{:S(2)}, u32[]{:S(2)}) collective-permute-start(f32[4,2,32,256]{3,2,1,0:T(8,128)} %get-tuple-element.64), channel_id=1, source_target_pairs={{0,4},{4,8},{8,12},{1,5},{5,9},{9,13},{2,6},{6,10},{10,14},{3,7},{... | collective-permute-start | bytes 786440 | tf_op jit(solution)/shard_map/ppermute | solution.py:21
  83.8 10.9 %collective-permute-start.7 = (f32[4,2,32,256]{3,2,1,0:T(8,128)}, f32[4,2,32,256]{3,2,1,0:T(8,128)}, u32[]{:S(2)}, u32[]{:S(2)}) collective-permute-start(f32[4,2,32,256]{3,2,1,0:T(8,128)} %get-tuple-element.65), channel_id=1, source_target_pairs={{4,0},{8,4},{12,8},{5,1},{9,5},{13,9},{6,2},{10,6},{14,10},{7,3},{... | collective-permute-start | bytes 786440 | tf_op jit(solution)/shard_map/ppermute | solution.py:24
  95.9 4.1 %collective-permute-start.8 = (f32[4,12,2,256]{3,2,1,0:T(2,128)S(1)}, f32[4,12,2,256]{3,2,1,0:T(2,128)S(1)}, u32[]{:S(2)}, u32[]{:S(2)}) collective-permute-start(f32[4,12,2,256]{3,2,1,0:T(2,128)S(1)} %get-tuple-element.56), channel_id=1, source_target_pairs={{0,2},{1,3},{4,6},{5,7},{8,10},{9,11},{12,14},{13,15},{16,18},{17,... | collective-permute-start | bytes 294920 | tf_op jit(solution)/shard_map/ppermute | solution.py:21
  97.4 6.7 %collective-permute-start.9 = (f32[4,12,2,256]{3,2,1,0:T(2,128)S(1)}, f32[4,12,2,256]{3,2,1,0:T(2,128)S(1)}, u32[]{:S(2)}, u32[]{:S(2)}) collective-permute-start(f32[4,12,2,256]{3,2,1,0:T(2,128)S(1)} %get-tuple-element.57), channel_id=1, source_target_pairs={{2,0},{3,1},{6,4},{7,5},{10,8},{11,9},{14,12},{15,13},{18,16},{19,... | collective-permute-start | bytes 294920 | tf_op jit(solution)/shard_map/ppermute | solution.py:24
  104.1 3.1 %copy-start.12 = (f32[4,12,2,256]{3,2,1,0:T(2,128)}, f32[4,12,2,256]{3,2,1,0:T(2,128)S(1)}, u32[]{:S(2)}) copy-start(f32[4,12,2,256]{3,2,1,0:T(2,128)S(1)} %collective-permute-done.9) | copy-start | bytes 294916
  108.8 8.1 %collective-permute-start.10 = (f32[4,12,36,2]{2,0,3,1:T(4,128)S(1)}, f32[4,12,36,2]{2,0,3,1:T(4,128)}, u32[]{:S(2)}, u32[]{:S(2)}) collective-permute-start(f32[4,12,36,2]{2,0,3,1:T(4,128)S(1)} %copy.28), channel_id=1, source_target_pairs={{0,1},{2,3},{4,5},{6,7},{8,9},{10,11},{12,13},{14,15},{16,17},{18,... | collective-permute-start | bytes 41480 | tf_op jit(solution)/shard_map/ppermute | solution.py:21
  113.0 6.2 %collective-permute-start.11 = (f32[4,12,36,2]{2,0,3,1:T(4,128)}, f32[4,12,36,2]{2,0,3,1:T(4,128)}, u32[]{:S(2)}, u32[]{:S(2)}) collective-permute-start(f32[4,12,36,2]{2,0,3,1:T(4,128)} %copy.29), channel_id=1, source_target_pairs={{1,0},{3,2},{5,4},{7,6},{9,8},{11,10},{13,12},{15,14},{17,16},{19,... | collective-permute-start | bytes 41480 | tf_op jit(solution)/shard_map/ppermute | solution.py:24
  124.9 3.8 %copy-start.3 = (f32[12,36,260]{2,1,0:T(8,128)}, f32[12,36,260]{2,1,0:T(8,128)S(1)}, u32[]{:S(2)}) copy-start(f32[12,36,260]{2,1,0:T(8,128)S(1)} %get-tuple-element.33) | copy-start | bytes 1347844
  130.8 1.2 copy-start.7
  130.8 1.2 copy-start.9
  130.8 1.2 copy-start.11
  132.0 1.6 copy-start.14
  132.0 1.6 copy-start.16
  133.1 62.5 %copy-start.4 = (f32[12,36,260]{2,1,0:T(8,128)S(1)}, f32[12,36,260]{2,1,0:T(8,128)}, u32[]{:S(2)}) copy-start(f32[12,36,260]{2,1,0:T(8,128)} %copy-done.3) | copy-start | bytes 1347844
where the time goes:
time: 228 us; the launch traced here: 227 us
  other arithmetic  89.2 us (39%)
  blocking collectives  60.5 us (27%)
  waiting for transfers between devices  27.4 us (12%)
  starting transfers between devices  24.9 us (11%)
  local copies, waits for them, and re-layouts  21.7 us (10%)
    psum x1, blocking collectives, local(): readings = lax.psum(partial_sum, ('slab', 'pencil', 'comp'))  60.5 us
    add x1, other arithmetic, advance(): damage_core + TIME_DAMAGE * (2.0 * (1.0 - damage_core) * energy - toughne...  31 us
    broadcast_in_dim x2, other arithmetic, local(): stacked = jnp.concatenate([moved, damage[None]], axis=0)  30.5 us
    ppermute x6, waiting for transfers between devices, with_halo(): lax.ppermute(lax.slice_in_dim(block, 0, width, axis=dim), axis, backward)  17.3 us
    ppermute x6, starting transfers between devices, with_halo(): lax.ppermute(lax.slice_in_dim(block, block.shape[dim] - width, None, axis...  17.2 us
    ppermute x6, waiting for transfers between devices, with_halo(): lax.ppermute(lax.slice_in_dim(block, block.shape[dim] - width, None, axis...  10.2 us
    mul x4, other arithmetic, advance(): total_force = total_force + central(degrade * stress, direction)  9.3 us
    concatenate x4, other arithmetic, with_halo(): block = jnp.concatenate([low, block, high], axis=dim)  8.23 us
  transfers between devices with their start and end apart: 12, of which 8 were waited for; matrix products, arithmetic and copies ran while one was open for 6% of the time, Pallas kernels for 0%

commit v1 on v0

--- a/solution.py
+++ b/solution.py
@@ -141,7 +141,7 @@
     picks = (block_ids[:, None] == sensor_cell[None, :]).astype(jnp.bfloat16)
     point = jnp.dot(pooled, picks, preferred_element_type=jnp.float32)
     partial_sum = dense + POINT_GAIN * point
-    readings = lax.psum(partial_sum, ("slab", "pencil", "comp"))
+    readings = jnp.sum(lax.all_gather(partial_sum, axis_name=("slab", "pencil", "comp")), axis=0)
     return (moved, damage, readings)
 
 

time: 228 us -> 192 us (0.84)
  blocking collectives: 60.5 us -> 23.5 us
    psum x1 -> x0, blocking collectives: 60.5 us -> none  [local(): readings = lax.psum(partial_sum, ('slab', 'pencil', 'comp'))]
    all_gather x0 -> x1, blocking collectives: none -> 23.5 us  [local(): lax.all_gather(partial_sum, axis_name=('slab', 'pencil', 'comp'))]
  transfers between devices with their start and end apart: 12 -> 12, of which waited for: 8 -> 8; matrix products, arithmetic and copies ran while one was open for 6% -> 7% of each run, Pallas kernels for 0% -> 0%
where the time goes in v1:
time: 192 us; the launch traced here: 191 us
  other arithmetic  91.3 us (48%)
  waiting for transfers between devices  27.4 us (14%)
  starting transfers between devices  24.9 us (13%)
  blocking collectives  23.5 us (12%)
  local copies, waits for them, and re-layouts  21.7 us (11%)
    add x1, other arithmetic, advance(): damage_core + TIME_DAMAGE * (2.0 * (1.0 - damage_core) * energy - toughne...  31 us
    broadcast_in_dim x2, other arithmetic, local(): stacked = jnp.concatenate([moved, damage[None]], axis=0)  30.5 us
    all_gather x1, blocking collectives, local(): lax.all_gather(partial_sum, axis_name=('slab', 'pencil', 'comp'))  23.5 us
    ppermute x6, waiting for transfers between devices, with_halo(): lax.ppermute(lax.slice_in_dim(block, 0, width, axis=dim), axis, backward)  17.3 us
    ppermute x6, starting transfers between devices, with_halo(): lax.ppermute(lax.slice_in_dim(block, block.shape[dim] - width, None, axis...  17.2 us
    ppermute x6, waiting for transfers between devices, with_halo(): lax.ppermute(lax.slice_in_dim(block, block.shape[dim] - width, None, axis...  10.1 us
    mul x4, other arithmetic, advance(): total_force = total_force + central(degrade * stress, direction)  9.34 us
    concatenate x4, other arithmetic, with_halo(): block = jnp.concatenate([low, block, high], axis=dim)  8.23 us
  transfers between devices with their start and end apart: 12, of which 8 were waited for; matrix products, arithmetic and copies ran while one was open for 7% of the time, Pallas kernels for 0%

profile of v1, /device:TPU:0, one launch (start us, length us, event | category | flops | bytes accessed | tf_op | source)
XLA Modules:
  0.0 190.9 jit_solution(16494714979199537831)
XLA Ops:
  2.9 5.0 %collective-permute-start = (f32[4,2,32,256]{3,2,1,0:T(8,128)S(1)}, f32[4,2,32,256]{3,2,1,0:T(8,128)S(1)}, u32[]{:S(2)}, u32[]{:S(2)}) collective-permute-start(f32[4,2,32,256]{3,2,1,0:T(8,128)S(1)} %get-tuple-element.66), channel_id=1, source_target_pairs={{0,4},{4,8},{8,12},{1,5},{5,9},{9,13},{2,6},{6,10},{10,14},{3,7},{... | collective-permute-start | bytes 786440 | tf_op jit(solution)/shard_map/ppermute | solution.py:21
  9.1 4.2 %collective-permute-done = f32[4,2,32,256]{3,2,1,0:T(8,128)S(1)} collective-permute-done((f32[4,2,32,256]{3,2,1,0:T(8,128)S(1)}, f32[4,2,32,256]{3,2,1,0:T(8,128)S(1)}, u32[]{:S(2)}, u32[]{:S(2)}) %collective-permute-start) | collective-permute-done | bytes 262176 | tf_op jit(solution)/shard_map/ppermute | solution.py:21
  13.4 4.1 %collective-permute-done.1 = f32[4,2,32,256]{3,2,1,0:T(8,128)S(1)} collective-permute-done((f32[4,2,32,256]{3,2,1,0:T(8,128)S(1)}, f32[4,2,32,256]{3,2,1,0:T(8,128)S(1)}, u32[]{:S(2)}, u32[]{:S(2)}) %collective-permute-start.1) | collective-permute-done | bytes 262176 | tf_op jit(solution)/shard_map/ppermute | solution.py:24
  18.7 3.4 %collective-permute-start.2 = (f32[4,12,2,256]{3,2,1,0:T(2,128)S(1)}, f32[4,12,2,256]{3,2,1,0:T(2,128)S(1)}, u32[]{:S(2)}, u32[]{:S(2)}) collective-permute-start(f32[4,12,2,256]{3,2,1,0:T(2,128)S(1)} %get-tuple-element.58), channel_id=1, source_target_pairs={{0,2},{1,3},{4,6},{5,7},{8,10},{9,11},{12,14},{13,15},{16,18},{17,... | collective-permute-start | bytes 294920 | tf_op jit(solution)/shard_map/ppermute | solution.py:21
  24.3 4.3 %collective-permute-done.3 = f32[4,12,2,256]{3,2,1,0:T(2,128)S(1)} collective-permute-done((f32[4,12,2,256]{3,2,1,0:T(2,128)S(1)}, f32[4,12,2,256]{3,2,1,0:T(2,128)S(1)}, u32[]{:S(2)}, u32[]{:S(2)}) %collective-permute-start.3) | collective-permute-done | bytes 98336 | tf_op jit(solution)/shard_map/ppermute | solution.py:24
  28.9 1.6 fusion.81
  30.5 1.6 copy.24
  32.2 1.9 collective-permute-start.4
  34.1 2.2 %copy.25 = f32[4,12,36,2]{2,0,3,1:T(4,128)} copy(f32[4,12,36,2]{3,2,1,0:T(8,128)} %get-tuple-element.55) | data formatting | bytes 27648 | tf_op jit(solution)/shard_map/slice | solution.py:24
  37.6 2.2 %copy.26 = f32[4,12,36,2]{3,2,1,0:T(8,128)} copy(f32[4,12,36,2]{2,0,3,1:T(4,128)} %collective-permute-done.4) | data formatting | bytes 27648 | tf_op jit(solution)/shard_map/ppermute | solution.py:21
  39.8 2.2 %copy.27 = f32[4,12,36,2]{3,2,1,0:T(8,128)} copy(f32[4,12,36,2]{2,0,3,1:T(4,128)} %collective-permute-done.5) | data formatting | bytes 27648 | tf_op jit(solution)/shard_map/ppermute | solution.py:24
  42.0 3.1 %pad_maximum_fusion = f32[4,12,36,260]{3,2,1,0:T(8,128)S(1)} fusion(f32[4,12,36,2]{3,2,1,0:T(8,128)} %copy.27, f32[4,12,2,256]{3,2,1,0:T(2,128)} %copy-done.13, f32[4,2,32,256]{3,2,1,0:T(8,128)} %copy-done.5, f32[1,8,32,256]{3,2,1,0:T(8,128)S(1)} %multiply_bitcast_fusion, f32[3,8,32,256]{3,2,1,0:T(8,128)S(1)} %copy-done.1, ...), kind=kLoop, calls=%fused_computation.4 | loop fusion | flops 3144960 | bytes 3594240 | tf_op jit(solution)/shard_map/concatenate | solution.py:25
  45.3 2.2 %multiply_multiply_fusion.5 = (f32[10,34,258]{2,1,0:T(8,128)S(1)}, f32[10,34,258]{2,1,0:T(8,128)S(1)}, f32[10,34,258]{2,1,0:T(8,128)S(1)}, f32[10,34,258]{2,1,0:...) fusion(f32[12,36,260]{2,1,0:T(8,128)S(1)} %get-tuple-element.37, ...), kind=kLoop, calls=%fused_computation.69 | loop fusion | flops 2456160 | bytes 8421120 | tf_op jit(solution)/shard_map/mul | solution.py:106
  50.1 29.3 %fusion.52 = f32[1,8,32,256]{3,2,1,0:T(8,128)S(1)} fusion(f32[8,32,256]{2,1,0:T(8,128)S(1)} %copy-done.15, f32[12,36,260]{2,1,0:T(8,128)S(1)} %get-tuple-element.37, f32[10,34,258]{2,1,0:T(8,128)S(1)} %get-tuple-element.46, f32[10,34,258]{2,1,0:T(8,128)S(1)} %get-tuple-element.47, f32[10,34,258]{2,1,0:T(8,128)S(1)} %get-tuple-element.29, ...), kind=kLoop, calls=%fused_computation.128 | loop fusion | flops 23068672 | bytes 4194304 | tf_op jit(solution)/shard_map/broadcast_in_dim | solution.py:128
  80.3 3.5 %collective-permute-start.6 = (f32[4,2,32,256]{3,2,1,0:T(8,128)}, f32[4,2,32,256]{3,2,1,0:T(8,128)S(1)}, u32[]{:S(2)}, u32[]{:S(2)}) collective-permute-start(f32[4,2,32,256]{3,2,1,0:T(8,128)} %get-tuple-element.64), channel_id=1, source_target_pairs={{0,4},{4,8},{8,12},{1,5},{5,9},{9,13},{2,6},{6,10},{10,14},{3,7},{... | collective-permute-start | bytes 786440 | tf_op jit(solution)/shard_map/ppermute | solution.py:21
  85.7 4.3 %collective-permute-done.6 = f32[4,2,32,256]{3,2,1,0:T(8,128)S(1)} collective-permute-done((f32[4,2,32,256]{3,2,1,0:T(8,128)}, f32[4,2,32,256]{3,2,1,0:T(8,128)S(1)}, u32[]{:S(2)}, u32[]{:S(2)}) %collective-permute-start.6) | collective-permute-done | bytes 262176 | tf_op jit(solution)/shard_map/ppermute | solution.py:21
  90.0 4.7 %collective-permute-done.7 = f32[4,2,32,256]{3,2,1,0:T(8,128)} collective-permute-done((f32[4,2,32,256]{3,2,1,0:T(8,128)}, f32[4,2,32,256]{3,2,1,0:T(8,128)}, u32[]{:S(2)}, u32[]{:S(2)}) %collective-permute-start.7) | collective-permute-done | bytes 262176 | tf_op jit(solution)/shard_map/ppermute | solution.py:24
  95.9 1.5 collective-permute-start.8
  100.0 4.1 %collective-permute-done.9 = f32[4,12,2,256]{3,2,1,0:T(2,128)S(1)} collective-permute-done((f32[4,12,2,256]{3,2,1,0:T(2,128)S(1)}, f32[4,12,2,256]{3,2,1,0:T(2,128)S(1)}, u32[]{:S(2)}, u32[]{:S(2)}) %collective-permute-start.9) | collective-permute-done | bytes 98336 | tf_op jit(solution)/shard_map/ppermute | solution.py:24
  104.1 1.5 pad_maximum_fusion.3
  105.6 1.6 fusion.80
  107.2 1.6 copy.28
  108.8 1.9 collective-permute-start.10
  110.7 2.2 %copy.29 = f32[4,12,36,2]{2,0,3,1:T(4,128)} copy(f32[4,12,36,2]{3,2,1,0:T(8,128)} %get-tuple-element.53) | data formatting | bytes 27648 | tf_op jit(solution)/shard_map/slice | solution.py:24
  116.9 2.2 %copy.30 = f32[4,12,36,2]{3,2,1,0:T(8,128)} copy(f32[4,12,36,2]{2,0,3,1:T(4,128)} %collective-permute-done.10) | data formatting | bytes 27648 | tf_op jit(solution)/shard_map/ppermute | solution.py:21
  119.1 2.2 %copy.31 = f32[4,12,36,2]{3,2,1,0:T(8,128)} copy(f32[4,12,36,2]{2,0,3,1:T(4,128)} %collective-permute-done.11) | data formatting | bytes 27648 | tf_op jit(solution)/shard_map/ppermute | solution.py:24
  121.3 3.3 %pad_maximum_fusion.1 = f32[4,12,36,260]{3,2,1,0:T(8,128)S(1)} fusion(f32[4,12,36,2]{3,2,1,0:T(8,128)} %copy.31, f32[4,12,2,256]{3,2,1,0:T(2,128)} %copy-done.12, f32[4,2,32,256]{3,2,1,0:T(8,128)} %collective-permute-done.7, f32[1,8,32,256]{3,2,1,0:T(8,128)S(1)} %fusion.52, f32[3,8,32,256]{3,2,1,0:T(8,128)} %copy-done.2, ...), kind=kLoop, calls=%fused_computation.5 | loop fusion | flops 3144960 | bytes 3594240 | tf_op jit(solution)/shard_map/concatenate | solution.py:25
  124.9 3.8 %multiply_multiply_fusion.2 = (f32[10,34,258]{2,1,0:T(8,128)S(1)}, f32[10,34,258]{2,1,0:T(8,128)}, f32[10,34,258]{2,1,0:T(8,128)S(1)}, f32[10,34,258]{2,1,0:T(8,...) fusion(f32[12,36,260]{2,1,0:T(8,128)S(1)} %get-tuple-element.33, ...), kind=kLoop, calls=%fused_computation.62 | loop fusion | flops 2456160 | bytes 8421120 | tf_op jit(solution)/shard_map/mul | solution.py:106
  128.7 2.1 %multiply_multiply_fusion = (f32[10,34,258]{2,1,0:T(8,128)S(1)}, f32[10,34,258]{2,1,0:T(8,128)}, f32[10,34,258]{2,1,0:T(8,128)S(1)}, f32[10,34,258]{2,1,0:T(8,128)S(1)}) fusion(f32[12,36,260]{2,1,0:T(8,128)S(1)} %get-tuple-element.33, f32[12,36,260]{2,1,0:T(8,128)S(1)} %get-tuple-element.30, f32[12,36,260]{2,1,0:T(8,128)S(1)} %get-tuple-element.31, ...), kind=kLoop, calls=%fused_computation.59 | loop fusion | flops 1666680 | bytes 4912320 | tf_op jit(solution)/shard_map/mul | solution.py:106
  134.4 23.5 %all-gather.1 = f32[16,3,4096]{2,1,0:T(4,128)} all-gather(f32[1,3,4096]{2,1,0:T(4,128)S(1)} %fusion.1), channel_id=2, replica_groups=mesh['groups'=2,'slab'=4,'pencil'=2,'comp'=2] {'slab','pencil','comp'}, dimensions={0}, use_global_device_ids=true | all-gather | bytes 835584 | tf_op jit(solution)/shard_map/all_gather | solution.py:144
  157.8 2.0 %reduce_sum.19 = f32[3,4096]{1,0:T(4,128)} reduce(f32[16,3,4096]{2,1,0:T(4,128)} %all-gather.1, f32[]{:T(128)} %constant.62.clone.1), dimensions={0}, to_apply=%region_1.0 | reduce | flops 184320 | bytes 835588 | tf_op jit(solution)/shard_map/reduce_sum | solution.py:144
  159.8 31.0 %fusion.27 = f32[8,32,256]{2,1,0:T(8,128)} fusion(f32[8,32,256]{2,1,0:T(8,128)} %param.6, f32[12,36,260]{2,1,0:T(8,128)S(1)} %copy-done.4, f32[10,34,258]{2,1,0:T(8,128)S(1)} %get-tuple-element.39, f32[10,34,258]{2,1,0:T(8,128)} %get-tuple-element.40, f32[10,34,258]{2,1,0:T(8,128)} %get-tuple-element.18, f32[10,34,258]{2,1,0:T(8,128)} %get-tuple-element.44, ...), kind=kLoop, calls=%fused_computation.83 | loop fusion | flops 23068672 | bytes 4194304 | tf_op jit(solution)/shard_map/add | solution.py:115
  (67 shorter events, 25.2 us)
Async XLA Ops:
  0.6 132.5 %copy-start = (bf16[8,32,1,4096]{3,1,2,0:T(8,128)(2,1)S(1)}, bf16[8,32,1,4096]{3,1,2,0:T(8,128)(2,1)}, u32[]{:S(2)}) copy-start(bf16[8,32,1,4096]{3,1,2,0:T(8,128)(2,1)} %param.8) | copy-start | bytes 6291460
  0.6 28.0 %copy-start.1 = (f32[3,8,32,256]{3,2,1,0:T(8,128)S(1)}, f32[3,8,32,256]{3,2,1,0:T(8,128)}, u32[]{:S(2)}) copy-start(f32[3,8,32,256]{3,2,1,0:T(8,128)} %param.5) | copy-start | bytes 2359300
  2.9 10.5 %collective-permute-start = (f32[4,2,32,256]{3,2,1,0:T(8,128)S(1)}, f32[4,2,32,256]{3,2,1,0:T(8,128)S(1)}, u32[]{:S(2)}, u32[]{:S(2)}) collective-permute-start(f32[4,2,32,256]{3,2,1,0:T(8,128)S(1)} %get-tuple-element.66), channel_id=1, source_target_pairs={{0,4},{4,8},{8,12},{1,5},{5,9},{9,13},{2,6},{6,10},{10,14},{3,7},{... | collective-permute-start | bytes 786440 | tf_op jit(solution)/shard_map/ppermute | solution.py:21
  7.8 9.7 %collective-permute-start.1 = (f32[4,2,32,256]{3,2,1,0:T(8,128)S(1)}, f32[4,2,32,256]{3,2,1,0:T(8,128)S(1)}, u32[]{:S(2)}, u32[]{:S(2)}) collective-permute-start(f32[4,2,32,256]{3,2,1,0:T(8,128)S(1)} %get-tuple-element.67), channel_id=1, source_target_pairs={{4,0},{8,4},{12,8},{5,1},{9,5},{13,9},{6,2},{10,6},{14,10},{7,3},{... | collective-permute-start | bytes 786440 | tf_op jit(solution)/shard_map/ppermute | solution.py:24
  17.5 13.0 %copy-start.5 = (f32[4,2,32,256]{3,2,1,0:T(8,128)}, f32[4,2,32,256]{3,2,1,0:T(8,128)S(1)}, u32[]{:S(2)}) copy-start(f32[4,2,32,256]{3,2,1,0:T(8,128)S(1)} %collective-permute-done.1) | copy-start | bytes 786436
  18.7 5.6 %collective-permute-start.2 = (f32[4,12,2,256]{3,2,1,0:T(2,128)S(1)}, f32[4,12,2,256]{3,2,1,0:T(2,128)S(1)}, u32[]{:S(2)}, u32[]{:S(2)}) collective-permute-start(f32[4,12,2,256]{3,2,1,0:T(2,128)S(1)} %get-tuple-element.58), channel_id=1, source_target_pairs={{0,2},{1,3},{4,6},{5,7},{8,10},{9,11},{12,14},{13,15},{16,18},{17,... | collective-permute-start | bytes 294920 | tf_op jit(solution)/shard_map/ppermute | solution.py:21
  22.1 6.5 %collective-permute-start.3 = (f32[4,12,2,256]{3,2,1,0:T(2,128)S(1)}, f32[4,12,2,256]{3,2,1,0:T(2,128)S(1)}, u32[]{:S(2)}, u32[]{:S(2)}) collective-permute-start(f32[4,12,2,256]{3,2,1,0:T(2,128)S(1)} %get-tuple-element.59), channel_id=1, source_target_pairs={{2,0},{3,1},{6,4},{7,5},{10,8},{11,9},{14,12},{15,13},{18,16},{19,... | collective-permute-start | bytes 294920 | tf_op jit(solution)/shard_map/ppermute | solution.py:24
  28.6 1.9 %copy-start.13 = (f32[4,12,2,256]{3,2,1,0:T(2,128)}, f32[4,12,2,256]{3,2,1,0:T(2,128)S(1)}, u32[]{:S(2)}) copy-start(f32[4,12,2,256]{3,2,1,0:T(2,128)S(1)} %collective-permute-done.3) | copy-start | bytes 294916
  32.2 5.4 %collective-permute-start.4 = (f32[4,12,36,2]{2,0,3,1:T(4,128)S(1)}, f32[4,12,36,2]{2,0,3,1:T(4,128)}, u32[]{:S(2)}, u32[]{:S(2)}) collective-permute-start(f32[4,12,36,2]{2,0,3,1:T(4,128)S(1)} %copy.24), channel_id=1, source_target_pairs={{0,1},{2,3},{4,5},{6,7},{8,9},{10,11},{12,13},{14,15},{16,17},{18,... | collective-permute-start | bytes 41480 | tf_op jit(solution)/shard_map/ppermute | solution.py:21
  36.3 3.5 %collective-permute-start.5 = (f32[4,12,36,2]{2,0,3,1:T(4,128)}, f32[4,12,36,2]{2,0,3,1:T(4,128)}, u32[]{:S(2)}, u32[]{:S(2)}) collective-permute-start(f32[4,12,36,2]{2,0,3,1:T(4,128)} %copy.25), channel_id=1, source_target_pairs={{1,0},{3,2},{5,4},{7,6},{9,8},{11,10},{13,12},{15,14},{17,16},{19,... | collective-permute-start | bytes 41480 | tf_op jit(solution)/shard_map/ppermute | solution.py:24
  48.8 1.3 copy-start.15
  49.9 29.5 %copy-start.6 = (f32[1,8,32,256]{3,2,1,0:T(8,128)}, f32[1,8,32,256]{3,2,1,0:T(8,128)S(1)}, u32[]{:S(2)}) copy-start(f32[1,8,32,256]{3,2,1,0:T(8,128)S(1)} %get-tuple-element.71) | copy-start | bytes 786436
  50.0 29.5 %copy-start.8 = (f32[1,8,32,256]{3,2,1,0:T(8,128)}, f32[1,8,32,256]{3,2,1,0:T(8,128)S(1)}, u32[]{:S(2)}) copy-start(f32[1,8,32,256]{3,2,1,0:T(8,128)S(1)} %get-tuple-element.72) | copy-start | bytes 786436
  50.0 29.5 %copy-start.10 = (f32[1,8,32,256]{3,2,1,0:T(8,128)}, f32[1,8,32,256]{3,2,1,0:T(8,128)S(1)}, u32[]{:S(2)}) copy-start(f32[1,8,32,256]{3,2,1,0:T(8,128)S(1)} %get-tuple-element.73) | copy-start | bytes 786436
  50.1 30.2 %copy-start.2 = (f32[3,8,32,256]{3,2,1,0:T(8,128)}, f32[3,8,32,256]{3,2,1,0:T(8,128)S(1)}, u32[]{:S(2)}) copy-start(f32[3,8,32,256]{3,2,1,0:T(8,128)S(1)} %fusion.5) | copy-start | bytes 2359300
  80.3 9.7 %collective-permute-start.6 = (f32[4,2,32,256]{3,2,1,0:T(8,128)}, f32[4,2,32,256]{3,2,1,0:T(8,128)S(1)}, u32[]{:S(2)}, u32[]{:S(2)}) collective-permute-start(f32[4,2,32,256]{3,2,1,0:T(8,128)} %get-tuple-element.64), channel_id=1, source_target_pairs={{0,4},{4,8},{8,12},{1,5},{5,9},{9,13},{2,6},{6,10},{10,14},{3,7},{... | collective-permute-start | bytes 786440 | tf_op jit(solution)/shard_map/ppermute | solution.py:21
  83.8 10.9 %collective-permute-start.7 = (f32[4,2,32,256]{3,2,1,0:T(8,128)}, f32[4,2,32,256]{3,2,1,0:T(8,128)}, u32[]{:S(2)}, u32[]{:S(2)}) collective-permute-start(f32[4,2,32,256]{3,2,1,0:T(8,128)} %get-tuple-element.65), channel_id=1, source_target_pairs={{4,0},{8,4},{12,8},{5,1},{9,5},{13,9},{6,2},{10,6},{14,10},{7,3},{... | collective-permute-start | bytes 786440 | tf_op jit(solution)/shard_map/ppermute | solution.py:24
  95.9 4.1 %collective-permute-start.8 = (f32[4,12,2,256]{3,2,1,0:T(2,128)S(1)}, f32[4,12,2,256]{3,2,1,0:T(2,128)S(1)}, u32[]{:S(2)}, u32[]{:S(2)}) collective-permute-start(f32[4,12,2,256]{3,2,1,0:T(2,128)S(1)} %get-tuple-element.56), channel_id=1, source_target_pairs={{0,2},{1,3},{4,6},{5,7},{8,10},{9,11},{12,14},{13,15},{16,18},{17,... | collective-permute-start | bytes 294920 | tf_op jit(solution)/shard_map/ppermute | solution.py:21
  97.4 6.6 %collective-permute-start.9 = (f32[4,12,2,256]{3,2,1,0:T(2,128)S(1)}, f32[4,12,2,256]{3,2,1,0:T(2,128)S(1)}, u32[]{:S(2)}, u32[]{:S(2)}) collective-permute-start(f32[4,12,2,256]{3,2,1,0:T(2,128)S(1)} %get-tuple-element.57), channel_id=1, source_target_pairs={{2,0},{3,1},{6,4},{7,5},{10,8},{11,9},{14,12},{15,13},{18,16},{19,... | collective-permute-start | bytes 294920 | tf_op jit(solution)/shard_map/ppermute | solution.py:24
  104.1 3.1 %copy-start.12 = (f32[4,12,2,256]{3,2,1,0:T(2,128)}, f32[4,12,2,256]{3,2,1,0:T(2,128)S(1)}, u32[]{:S(2)}) copy-start(f32[4,12,2,256]{3,2,1,0:T(2,128)S(1)} %collective-permute-done.9) | copy-start | bytes 294916
  108.8 8.1 %collective-permute-start.10 = (f32[4,12,36,2]{2,0,3,1:T(4,128)S(1)}, f32[4,12,36,2]{2,0,3,1:T(4,128)}, u32[]{:S(2)}, u32[]{:S(2)}) collective-permute-start(f32[4,12,36,2]{2,0,3,1:T(4,128)S(1)} %copy.28), channel_id=1, source_target_pairs={{0,1},{2,3},{4,5},{6,7},{8,9},{10,11},{12,13},{14,15},{16,17},{18,... | collective-permute-start | bytes 41480 | tf_op jit(solution)/shard_map/ppermute | solution.py:21
  112.9 6.2 %collective-permute-start.11 = (f32[4,12,36,2]{2,0,3,1:T(4,128)}, f32[4,12,36,2]{2,0,3,1:T(4,128)}, u32[]{:S(2)}, u32[]{:S(2)}) collective-permute-start(f32[4,12,36,2]{2,0,3,1:T(4,128)} %copy.29), channel_id=1, source_target_pairs={{1,0},{3,2},{5,4},{7,6},{9,8},{11,10},{13,12},{15,14},{17,16},{19,... | collective-permute-start | bytes 41480 | tf_op jit(solution)/shard_map/ppermute | solution.py:24
  124.9 3.8 %copy-start.3 = (f32[12,36,260]{2,1,0:T(8,128)}, f32[12,36,260]{2,1,0:T(8,128)S(1)}, u32[]{:S(2)}) copy-start(f32[12,36,260]{2,1,0:T(8,128)S(1)} %get-tuple-element.33) | copy-start | bytes 1347844
  130.8 1.2 copy-start.7
  130.8 1.2 copy-start.9
  130.8 1.2 copy-start.11
  132.0 1.6 copy-start.14
  132.0 1.6 copy-start.16
  133.1 26.8 %copy-start.4 = (f32[12,36,260]{2,1,0:T(8,128)S(1)}, f32[12,36,260]{2,1,0:T(8,128)}, u32[]{:S(2)}) copy-start(f32[12,36,260]{2,1,0:T(8,128)} %copy-done.3) | copy-start | bytes 1347844
